TPU v7x, 8 devices: a whole 2x2x1 slice. The times are simulated.
8 devices in a mesh: dp: 1 (over z), kvh: 2 (over y), seq: 4 (over x, core).
Axes of the slice: x: 2, y: 2, z: 1, core: 2. Of those that a mesh axis runs over, the one named last changes fastest.
Arguments:
- x_hidden: bfloat16 [128, 6144], P('dp')
- seq_lens: int32 [128], P('dp')
- k_cache: bfloat16 [128, 2048, 8, 128], P('dp', 'seq', 'kvh')
- v_cache: bfloat16 [128, 2048, 8, 128], P('dp', 'seq', 'kvh')
- w_q: bfloat16 [6144, 48, 128], P(None, ('kvh', 'seq'))
- w_o: bfloat16 [48, 128, 6144], P(('kvh', 'seq'))
Outputs:
- output: bfloat16 [128, 6144], P('dp')
All inputs are finite; a program needn't handle non-finite values.
Results may differ from a plain program's by a relative error of at most 0.00348738.
Values are sent between devices in bfloat16 or wider.
A program may use at most 1 GiB of HBM per device.

v0:
```python
import jax
import jax.numpy as jnp
from jax import lax
from jax.sharding import PartitionSpec as P

ROPE_THETA = 500000.0
NEG_FILL = -1e30


def rotate_query(q_raw, seq_lens):
    half_dim = q_raw.shape[-1] // 2
    inv_freq = jnp.power(ROPE_THETA, -jnp.arange(half_dim, dtype=jnp.float32) * (2.0 / q_raw.shape[-1]))
    angle = (seq_lens - 1).astype(jnp.float32)[:, None] * inv_freq[None, :]
    cosine = jnp.cos(angle)[:, None, :]
    sine = jnp.sin(angle)[:, None, :]
    first = q_raw[..., :half_dim]
    second = q_raw[..., half_dim:]
    return jnp.concatenate([first * cosine - second * sine, second * cosine + first * sine], axis=-1)


def solution(mesh):
    def local_step(x_hidden, seq_lens, k_loc, v_loc, wq_loc, wo_loc):
        row_count = x_hidden.shape[0]
        t_dev = k_loc.shape[1]
        kv_loc = k_loc.shape[2]
        head_dim = k_loc.shape[3]
        q_raw = jnp.einsum('bd,dhk->bhk', x_hidden, wq_loc, preferred_element_type=jnp.float32)
        q_own = rotate_query(q_raw, seq_lens).astype(jnp.bfloat16)
        q_slice = lax.all_gather(q_own, 'seq', axis=1, tiled=True)
        slice_heads = q_slice.shape[1]
        q_grp = q_slice.reshape(row_count, kv_loc, slice_heads // kv_loc, head_dim)
        scores = jnp.einsum('bngk,btnk->bngt', q_grp, k_loc, preferred_element_type=jnp.float32) * (head_dim ** -0.5)
        positions = lax.axis_index('seq') * t_dev + jnp.arange(t_dev)
        valid_mask = (positions[None, :] < seq_lens[:, None])[:, None, None, :]
        scores = jnp.where(valid_mask, scores, NEG_FILL)
        local_max = jnp.max(scores, axis=-1)
        weights = jnp.where(valid_mask, jnp.exp(scores - local_max[..., None]), 0.0)
        local_sum = jnp.sum(weights, axis=-1)
        local_out = jnp.einsum('bngt,btnk->bngk', weights.astype(jnp.bfloat16), v_loc, preferred_element_type=jnp.float32)
        global_max = lax.pmax(local_max, 'seq')
        rescale = jnp.exp(local_max - global_max)
        out_part = (local_out * rescale[..., None]).reshape(row_count, slice_heads, head_dim)
        sum_part = (local_sum * rescale).reshape(row_count, slice_heads)
        out_own = lax.psum_scatter(out_part, 'seq', scatter_dimension=1, tiled=True)
        sum_own = lax.psum_scatter(sum_part, 'seq', scatter_dimension=1, tiled=True)
        attn = (out_own / sum_own[..., None]).astype(jnp.bfloat16)
        y_part = jnp.einsum('bhk,hkd->bd', attn, wo_loc, preferred_element_type=jnp.float32)
        y_sum = lax.psum(y_part, ('kvh', 'seq'))
        return (x_hidden.astype(jnp.float32) + y_sum).astype(jnp.bfloat16)

    return jax.shard_map(
        local_step,
        mesh=mesh,
        in_specs=(P('dp', None), P('dp'), P('dp', 'seq', 'kvh', None), P('dp', 'seq', 'kvh', None),
                  P(None, ('kvh', 'seq'), None), P(('kvh', 'seq'), None, None)),
        out_specs=P('dp', None),
        check_vma=False)
```

profile of v0, /device:TPU:0, one launch (start us, length us, event | category | flops | bytes accessed | tf_op | source)
XLA Modules:
  0.0 220.9 jit_solution(14940422986517114560)
XLA Ops:
  6.5 0.0 reduce-scatter.2.cloned.1.call-start
  6.6 0.7 add_convert_fusion.2
  7.2 0.0 copy-start
  7.2 12.8 %copy.27 = bf16[6144,6,128]{0,2,1:T(8,128)(2,1)} copy(bf16[6144,6,128]{2,0,1:T(8,128)(2,1)} %param.10) | data formatting | bytes 18874368 | tf_op args[4]
  20.0 0.2 multiply_cosine_fusion
  20.2 0.0 copy-done
  20.2 0.0 copy-start.1
  20.2 5.2 %fusion.24 = f32[128,768]{0,1:S(1)} fusion(bf16[128,6144]{1,0:T(8,128)(2,1)S(1)} %copy-done, bf16[6144,768]{0,1:T(8,128)(2,1)} %bitcast.17), kind=kOutput, calls=%fused_computation.35 | convolution fusion | flops 1207959552 | bytes 11403264
  25.4 0.1 subtract_convert_fusion
  25.5 0.2 copy.28
  25.7 13.0 %all_gather.3 = bf16[128,24,128]{2,0,1:T(8,128)(2,1)S(1)} all-gather(bf16[128,6,128]{2,0,1:T(8,128)(2,1)S(1)} %copy.28), channel_id=1, replica_groups=mesh['dp'=1,'kvh'=2,'seq'=4] {'seq'}, dimensions={1}, use_global_device_ids=true | all-gather | bytes 983040 | tf_op jit(solution)/shard_map/all_gather | solution.py:29
  38.7 0.0 copy-done.1
  38.7 0.1 broadcast_compare_fusion
  38.8 29.9 %fusion.4 = (f32[128,4,6]{2,1,0:T(4,128)S(1)}, f32[128,4,6,512]{3,2,1,0:T(8,128)}) fusion(pred[128,512]{1,0:T(8,128)(4,1)S(1)} %broadcast_compare_fusion, bf16[128,512,4,128]{3,2,1,0:T(4,128)(2,1)} %param.8, bf16[128,4,6,128]{3,0,2,1:T(8,128)(2,1)S(1)} %bitcast.19), kind=kOutput, calls=%fused_computation.7 | convolution fusion | flops 407368704 | bytes 74264576 | tf_op jit(solution)/shard_map/bngk,btnk->bngt/dot_general | solution.py:32
  68.7 14.5 %pmax.7 = f32[128,4,6]{2,1,0:T(4,128)S(1)} all-reduce(f32[128,4,6]{2,1,0:T(4,128)S(1)} %get-tuple-element.11), channel_id=1, replica_groups=mesh['dp'=1,'kvh'=2,'seq'=4] {'seq'}, use_global_device_ids=true, to_apply=%region_1.2 | all-reduce | flops 3072 | bytes 24576 | tf_op jit(solution)/shard_map/pmax | solution.py:40
  83.2 6.5 %fusion.5 = f32[128,4,6]{2,1,0:T(4,128)S(1)} fusion(f32[128,4,6,512]{3,2,1,0:T(8,128)} %get-tuple-element.12, f32[128,4,6]{2,1,0:T(4,128)S(1)} %get-tuple-element.11, pred[128,512]{1,0:T(8,128)(4,1)S(1)} %broadcast_compare_fusion), kind=kLoop, calls=%fused_computation.8 | loop fusion | flops 7861248 | bytes 6381568 | tf_op jit(solution)/shard_map/reduce_sum | solution.py:38
  89.7 0.1 fusion.23
  89.8 0.0 copy-start.2
  89.8 29.3 %fusion.13 = f32[128,4,6,128]{3,2,1,0:T(8,128)} fusion(bf16[128,512,4,128]{3,2,1,0:T(4,128)(2,1)} %param.9, f32[128,4,6,512]{3,2,1,0:T(8,128)} %get-tuple-element.12, f32[128,4,6]{2,1,0:T(4,128)S(1)} %get-tuple-element.11, pred[128,512]{1,0:T(8,128)(4,1)S(1)} %broadcast_compare_fusion, f32[128,4,6]{2,1,0:T(4,128)S(1)} %bitcast.25), kind=kOutput, calls=%fused_computation.16 | convolution fusion | flops 410910720 | bytes 75063296 | tf_op jit(solution)/shard_map/bngt,btnk->bngk/dot_general | solution.py:39
  119.1 3.6 %copy.32 = f32[128,4,6,128]{3,0,2,1:T(8,128)} copy(f32[128,4,6,128]{3,2,1,0:T(8,128)} %fusion.13) | data formatting | bytes 3145728 | tf_op jit(solution)/shard_map/mul | solution.py:42
  122.7 0.0 reduce-scatter.2.cloned.1.call-update
  122.8 0.0 all-reduce.3.cloned.1.call-start
  122.8 0.1 copy.33
  122.9 0.0 copy-done.2
  122.9 0.7 dynamic-slice
  124.3 10.1 %all-reduce = f32[128,24]{0,1:T(8,128)S(1)} all-reduce(f32[128,24]{0,1:T(8,128)S(1)} %reshape.92), channel_id=3, replica_groups=mesh['dp'=1,'kvh'=2,'seq'=4] {'seq'}, use_global_device_ids=true, to_apply=%region_4.5.clone | all-reduce | flops 3072 | bytes 24576
  134.4 11.1 %reduce-scatter.2.cloned.1.call-done = f32[128,6,128]{2,0,1:T(8,128)} async-done(((f32[128,24,128]{2,0,1:T(8,128)}), f32[128,6,128]{2,0,1:T(8,128)}) %reduce-scatter.2.cloned.1.call-update) | async-done | bytes 393232 | tf_op jit(solution)/shard_map/reduce_scatter | solution.py:44
  145.5 6.9 %convolution_bitcast_fusion = f32[128,6144]{1,0:T(8,128)} fusion(bf16[6,128,6144]{2,1,0:T(8,128)(2,1)} %param.11, f32[128,6,128]{2,0,1:T(8,128)} %reduce-scatter.2.cloned.1.call-done, f32[128,6]{0,1:T(8,128)S(1)} %constant_dynamic-slice_fusion), kind=kOutput, calls=%fused_computation.6 | convolution fusion | flops 1208156160 | bytes 12979200 | tf_op jit(solution)/shard_map/bhk,hkd->bd/dot_general | solution.py:47
  152.4 0.0 all-reduce.3.cloned.1.call-update
  152.5 58.2 %all-reduce.3.cloned.1.call-done = f32[128,6144]{1,0:T(8,128)} async-done(((f32[128,6144]{1,0:T(8,128)}), f32[128,6144]{1,0:T(8,128)}) %all-reduce.3.cloned.1.call-update) | async-done | bytes 3145744 | tf_op jit(solution)/shard_map/psum | solution.py:48
  210.7 3.3 %add_convert_fusion = bf16[128,6144]{1,0:T(8,128)(2,1)} fusion(f32[128,6144]{1,0:T(8,128)} %all-reduce.3.cloned.1.call-done, bf16[128,6144]{1,0:T(8,128)(2,1)S(1)} %copy-done), kind=kLoop, calls=%fused_computation.15 | loop fusion | flops 2359296 | bytes 6291456 | tf_op jit(solution)/shard_map/convert_element_type | solution.py:49
  (5 shorter events, 0.0 us)
Async XLA Ops:
  6.5 139.0 %reduce-scatter.2.cloned.1.call-start = ((), (), s32[]{:S(2)}) async-start(), calls=%async_computation.1 | async-start | bytes 1966080 | tf_op jit(solution)/shard_map/reduce_scatter | solution.py:44
  7.2 13.0 %copy-start = (bf16[128,6144]{1,0:T(8,128)(2,1)S(1)}, bf16[128,6144]{1,0:T(8,128)(2,1)}, u32[]{:S(2)}) copy-start(bf16[128,6144]{1,0:T(8,128)(2,1)} %param.6) | copy-start | bytes 4718596
  20.2 18.5 %copy-start.1 = (s32[128]{0:T(128)S(1)}, s32[128]{0:T(128)}, u32[]{:S(2)}) copy-start(s32[128]{0:T(128)} %param.7) | copy-start | bytes 1540
  89.8 33.1 %copy-start.2 = (u32[8]{0:T(128)S(1)}, u32[8]{0:T(128)}, u32[]{:S(2)}) copy-start(u32[8]{0:T(128)} %constant.25) | copy-start | bytes 100
  122.8 87.9 %all-reduce.3.cloned.1.call-start = ((), (), s32[]{:S(2)}) async-start(), calls=%async_computation.2 | async-start | bytes 6291456 | tf_op jit(solution)/shard_map/psum | solution.py:48
Sparse Core Ops, SparseCore 0:
  122.9 22.5 reduce-scatter.1
  152.6 58.0 all-reduce.2
where the time goes:
time: 221 us
  matrix products  71.3 us (32%)
  waiting for transfers between devices  69.3 us (31%)
  blocking collectives  37.6 us (17%)
  local copies, waits for them, and re-layouts  17.4 us (8%)
  between operations  14.2 us (6%)
  other arithmetic  10.9 us (5%)
    psum x1, waiting for transfers between devices, local_step(): y_sum = lax.psum(y_part, ('kvh', 'seq'))  58.2 us
    dot_general x1, matrix products, local_step(): jnp.einsum('bngk,btnk->bngt', q_grp, k_loc, preferred_element_type=jnp.fl...  29.9 us
    dot_general x1, matrix products, local_step(): jnp.einsum('bngt,btnk->bngk', weights.astype(jnp.bfloat16), v_loc, prefer...  29.3 us
    pmax x1, blocking collectives, local_step(): global_max = lax.pmax(local_max, 'seq')  14.5 us
    unnamed x9, local copies, waits for them, and re-layouts  13.5 us
    all_gather x1, blocking collectives, local_step(): q_slice = lax.all_gather(q_own, 'seq', axis=1, tiled=True)  13 us
    reduce_scatter x1, waiting for transfers between devices, local_step(): out_own = lax.psum_scatter(out_part, 'seq', scatter_dimension=1, tiled=True)  11.1 us
    unnamed x1, blocking collectives  10.1 us
  transfers between devices with their start and end apart: 2, of which 2 were waited for; matrix products, arithmetic and copies ran while one was open for 0% of the time, Pallas kernels for 0%

commit v1 on v0

v1 whole, which is shorter than its diff:
```python
import functools

import jax
import jax.numpy as jnp
from jax import lax
from jax.experimental import pallas as pl
from jax.experimental.pallas import tpu as pltpu
from jax.sharding import PartitionSpec as P

ROPE_THETA = 500000.0
HEAD_DIM = 128
NEG = -3.3e38
FLOOR = -3.0e38
LOG2E = 1.4426950408889634
SCALE2 = HEAD_DIM ** -0.5 * LOG2E
SLOTS = 16
UNROLL = 2


def rope_tables(seq_lens):
    half_dim = HEAD_DIM // 2
    inv_freq = jnp.power(ROPE_THETA, -jnp.arange(half_dim, dtype=jnp.float32) * (2.0 / HEAD_DIM))
    angle = (seq_lens - 1).astype(jnp.float32)[:, None] * inv_freq[None, :]
    return jnp.cos(angle), jnp.sin(angle)


def head_lanes(width):
    lane = lax.broadcasted_iota(jnp.int32, (8, width), 1)
    return lane, [lane % 4 == n for n in range(4)]


def pick(masks, parts):
    return jnp.where(masks[0], parts[0], jnp.where(masks[1], parts[1], jnp.where(masks[2], parts[2], parts[3])))


def score_row(q32, k_at, limit, p_at, stat_at):
    tiles = k_at.shape[0] // 512
    zero = jnp.zeros_like(q32)
    q_diag = jnp.concatenate([jnp.concatenate([q32, zero], 1), jnp.concatenate([zero, q32], 1)], 0)
    lane, masks = head_lanes(256)
    scores = []
    for j in range(tiles):
        keys = jnp.concatenate([k_at[pl.ds(512 * j, 256), :], k_at[pl.ds(512 * j + 256, 256), :]], 1)
        s = lax.dot_general(q_diag, keys, (((1,), (1,)), ((), ())), preferred_element_type=jnp.float32)
        for h in range(2):
            mine = pick(masks, [s[32 * h + 8 * n:32 * h + 8 * n + 8] for n in range(4)])
            scores.append(jnp.where(lane < limit - (512 * j + 256 * h), mine, NEG))
    top = functools.reduce(jnp.maximum, scores)
    top = jnp.maximum(top[:, :128], top[:, 128:])
    _, half = head_lanes(128)
    tops = [jnp.maximum(jnp.max(jnp.where(half[n], top, NEG), axis=1, keepdims=True), FLOOR) * SCALE2 for n in range(4)]
    shift = pick(half, tops)
    shift = jnp.concatenate([shift, shift], 1)
    total = None
    for j in range(tiles):
        rows = []
        for h in range(2):
            w = jnp.exp2(scores[2 * j + h] * SCALE2 - shift)
            total = w if total is None else total + w
            rows += [jnp.where(masks[n], w, 0.0) for n in range(4)]
        p_at[j] = jnp.concatenate(rows, 0).astype(jnp.bfloat16)
    total = total[:, :128] + total[:, 128:]
    row = lax.broadcasted_iota(jnp.int32, (8, 128), 0)
    lane128 = lax.broadcasted_iota(jnp.int32, (8, 128), 1)
    diagonal = row == lane128
    for n in range(4):
        sums = jnp.sum(jnp.where(half[n], total, 0.0), axis=1, keepdims=True)
        top_row = jnp.sum(jnp.where(diagonal, tops[n], 0.0), axis=0, keepdims=True)
        sum_row = jnp.sum(jnp.where(diagonal, sums, 0.0), axis=0, keepdims=True)
        stat_at[n] = jnp.where(row == 6, top_row, sum_row)


def value_row(p_at, v_at, stat_at, out_at):
    tiles = v_at.shape[0] // 512
    acc = None
    for j in range(tiles):
        values = jnp.concatenate([v_at[pl.ds(512 * j, 256), :], v_at[pl.ds(512 * j + 256, 256), :]], 1)
        o = jnp.dot(p_at[j], values, preferred_element_type=jnp.float32)
        acc = o if acc is None else acc + o
    row = lax.broadcasted_iota(jnp.int32, (8, 128), 0)
    for n in range(4):
        o = acc[8 * n:8 * n + 8, :128] + acc[32 + 8 * n:40 + 8 * n, 128:]
        out_at[n] = jnp.where(row < 6, o, stat_at[n])


def attend_kernel(lens_ref, q_ref, k_hbm, v_hbm, out_ref, k_buf, v_buf, p_buf, stat_buf, k_sem, v_sem):
    rows = q_ref.shape[0]
    depth = k_buf.shape[1]
    base = lax.axis_index('seq') * depth

    def k_copy(r):
        slot = lax.rem(r, SLOTS)
        return pltpu.make_async_copy(k_hbm.at[r], k_buf.at[slot], k_sem.at[slot])

    def v_copy(r):
        slot = lax.rem(r, SLOTS)
        return pltpu.make_async_copy(v_hbm.at[r], v_buf.at[slot], v_sem.at[slot])

    def prime(r, c):
        k_copy(r).start()
        v_copy(r).start()
        return c
    lax.fori_loop(0, SLOTS, prime, 0)

    def step(i, c):
        first = i * UNROLL
        parity = lax.rem(i, 2)
        for u in range(UNROLL):
            k_copy(first + u).wait()
        back = first - UNROLL
        for u in range(UNROLL):
            @pl.when(i > 0)
            def _():
                v_copy(back + u).wait()
        for u in range(UNROLL):
            limit = lens_ref[first + u] * 4 - base
            score_row(q_ref[first + u], k_buf.at[lax.rem(first + u, SLOTS)], limit,
                      p_buf.at[parity, u], stat_buf.at[parity, u])
            r = lax.max(back + u, 0)
            value_row(p_buf.at[1 - parity, u], v_buf.at[lax.rem(r, SLOTS)], stat_buf.at[1 - parity, u],
                      out_ref.at[r])
        for u in range(UNROLL):
            @pl.when(first + u + SLOTS < rows)
            def _():
                k_copy(first + u + SLOTS).start()

            @pl.when((i > 0) & (back + u + SLOTS < rows))
            def _():
                v_copy(back + u + SLOTS).start()
        return c
    steps = rows // UNROLL
    lax.fori_loop(0, steps, step, 0)
    for u in range(UNROLL):
        r = rows - UNROLL + u
        v_copy(r).wait()
        value_row(p_buf.at[(steps - 1) % 2, u], v_buf.at[r % SLOTS], stat_buf.at[(steps - 1) % 2, u], out_ref.at[r])


def attend(seq_lens, q_all, k_loc, v_loc):
    rows, depth = k_loc.shape[0], k_loc.shape[1]
    return pl.pallas_call(
        attend_kernel,
        out_shape=jax.ShapeDtypeStruct((rows, 4, 8, HEAD_DIM), jnp.float32),
        in_specs=[pl.BlockSpec(memory_space=pltpu.SMEM), pl.BlockSpec(memory_space=pltpu.VMEM),
                  pl.BlockSpec(memory_space=pl.ANY), pl.BlockSpec(memory_space=pl.ANY)],
        out_specs=pl.BlockSpec(memory_space=pltpu.VMEM),
        scratch_shapes=[
            pltpu.VMEM((SLOTS, depth, HEAD_DIM), jnp.bfloat16),
            pltpu.VMEM((SLOTS, depth, HEAD_DIM), jnp.bfloat16),
            pltpu.VMEM((2, UNROLL, depth // 512, 64, 256), jnp.bfloat16),
            pltpu.VMEM((2, UNROLL, 4, 8, HEAD_DIM), jnp.float32),
            pltpu.SemaphoreType.DMA((SLOTS,)),
            pltpu.SemaphoreType.DMA((SLOTS,)),
        ],
        compiler_params=pltpu.CompilerParams(vmem_limit_bytes=50 * 2 ** 20),
    )(seq_lens, q_all, k_loc, v_loc)


def solution(mesh):
    def local_step(x_hidden, seq_lens, k_loc, v_loc, wq_loc, wo_loc):
        rows, t_dev, kv_loc, head_dim = k_loc.shape
        q_raw = jnp.einsum('bd,dhk->bhk', x_hidden, wq_loc, preferred_element_type=jnp.float32)
        cosine, sine = rope_tables(seq_lens)
        cosine, sine = cosine[:, None, :], sine[:, None, :]
        first, second = q_raw[..., :head_dim // 2], q_raw[..., head_dim // 2:]
        q_own = jnp.concatenate([first * cosine - second * sine, second * cosine + first * sine], axis=-1).astype(jnp.bfloat16)
        q_all = lax.all_gather(q_own, 'seq', axis=1, tiled=True).reshape(rows, kv_loc, 6, head_dim)
        q_all = jnp.pad(q_all, ((0, 0), (0, 0), (0, 2), (0, 0))).reshape(rows, kv_loc * 8, head_dim)
        part = attend(seq_lens, q_all, k_loc.reshape(rows, t_dev * kv_loc, head_dim),
                      v_loc.reshape(rows, t_dev * kv_loc, head_dim))
        local_max = part[:, :, 6, :6]
        local_sum = part[:, :, 7, :6]
        global_max = lax.pmax(local_max, 'seq')
        rescale = jnp.exp2(local_max - global_max)
        out_own = lax.psum_scatter(part[:, :, :6] * rescale[..., None], 'seq', scatter_dimension=1, tiled=True)
        sum_own = lax.psum_scatter(local_sum * rescale, 'seq', scatter_dimension=1, tiled=True)
        attn = (out_own / sum_own[..., None]).astype(jnp.bfloat16).reshape(rows, 6, head_dim)
        y_part = jnp.einsum('bhk,hkd->bd', attn, wo_loc, preferred_element_type=jnp.float32)
        y_sum = lax.psum(y_part, ('kvh', 'seq'))
        return (x_hidden.astype(jnp.float32) + y_sum).astype(jnp.bfloat16)

    return jax.shard_map(
        local_step,
        mesh=mesh,
        in_specs=(P('dp', None), P('dp'), P('dp', 'seq', 'kvh', None), P('dp', 'seq', 'kvh', None),
                  P(None, ('kvh', 'seq'), None), P(('kvh', 'seq'), None, None)),
        out_specs=P('dp', None),
        check_vma=False)
```

time: 221 us -> 229 us (1.036)
  Pallas kernels: 0 us -> 73.5 us
  matrix products: 71.3 us -> 12.1 us
  other arithmetic: 10.9 us -> 4.54 us
    pallas_call x0 -> x1, Pallas kernels: none -> 73.5 us  [attend(): pl.pallas_call(attend_kernel, out_shape=jax.ShapeDtypeStruct((rows, 4, 8,...]
    dot_general x2 -> x0, matrix products: 59.2 us -> none  [the longest x1 29.9 us: local_step(): jnp.einsum('bngk,btnk->bngt', q_grp, k_loc, preferred_element_type=jnp.fl...]
    unnamed x2 -> x3, waiting for transfers between devices: 0.03 us -> 11.2 us
    reduce_scatter x1 -> x0, waiting for transfers between devices: 11.1 us -> none  [local_step(): out_own = lax.psum_scatter(out_part, 'seq', scatter_dimension=1, tiled=True)]
    reduce_sum x1 -> x0, other arithmetic: 6.48 us -> none  [local_step(): local_sum = jnp.sum(weights, axis=-1)]
    unnamed x9 -> x10, local copies, waits for them, and re-layouts: 13.5 us -> 13.5 us
  transfers between devices with their start and end apart: 2 -> 2, of which waited for: 2 -> 2; matrix products, arithmetic and copies ran while one was open for 0% -> 1% of each run, Pallas kernels for 0% -> 0%
where the time goes in v1:
time: 229 us; the launch traced here: 228 us
  Pallas kernels  73.5 us (32%)
  waiting for transfers between devices  69.4 us (30%)
  blocking collectives  37.4 us (16%)
  local copies, waits for them, and re-layouts  17.6 us (8%)
  between operations  13.5 us (6%)
  matrix products  12.1 us (5%)
  other arithmetic  4.54 us (2%)
    pallas_call x1, Pallas kernels, attend(): pl.pallas_call(attend_kernel, out_shape=jax.ShapeDtypeStruct((rows, 4, 8,...  73.5 us
    psum x1, waiting for transfers between devices, local_step(): y_sum = lax.psum(y_part, ('kvh', 'seq'))  58.2 us
    pmax x1, blocking collectives, local_step(): global_max = lax.pmax(local_max, 'seq')  14.3 us
    unnamed x10, local copies, waits for them, and re-layouts  13.5 us
    all_gather x1, blocking collectives, local_step(): lax.all_gather(q_own, 'seq', axis=1, tiled=True)  13 us
    unnamed x3, waiting for transfers between devices  11.2 us
    unnamed x1, blocking collectives  10.1 us
    dot_general x1, matrix products, local_step(): jnp.einsum('bhk,hkd->bd', attn, wo_loc, preferred_element_type=jnp.float32)  6.93 us
  transfers between devices with their start and end apart: 2, of which 2 were waited for; matrix products, arithmetic and copies ran while one was open for 1% of the time, Pallas kernels for 0%

profile of v1, /device:TPU:0, one launch (start us, length us, event | category | flops | bytes accessed | tf_op | source)
XLA Modules:
  0.0 228.3 jit_solution(4629136430984777070)
XLA Ops:
  6.5 0.0 reduce-scatter.4.cloned.1.call-start
  6.5 0.0 copy-start
  6.6 0.0 copy-start.1
  6.6 12.8 %copy.11 = bf16[6144,6,128]{0,2,1:T(8,128)(2,1)} copy(bf16[6144,6,128]{2,0,1:T(8,128)(2,1)} %param.10) | data formatting | bytes 18874368 | tf_op args[4]
  19.4 0.0 copy-done
  19.4 0.0 copy-done.1
  19.4 5.2 %fusion.3 = f32[128,768]{0,1:S(1)} fusion(bf16[128,6144]{1,0:T(8,128)(2,1)S(1)} %copy-done.1, bf16[6144,768]{0,1:T(8,128)(2,1)} %bitcast.22), kind=kOutput, calls=%fused_computation.17 | convolution fusion | flops 1207959552 | bytes 11403264
  24.6 0.2 multiply_cosine_fusion
  24.8 0.1 subtract_convert_fusion
  24.9 0.2 copy.12
  25.1 13.0 %all_gather.3 = bf16[128,24,128]{2,0,1:T(8,128)(2,1)S(1)} all-gather(bf16[128,6,128]{2,0,1:T(8,128)(2,1)S(1)} %copy.12), channel_id=1, replica_groups=mesh['dp'=1,'kvh'=2,'seq'=4] {'seq'}, dimensions={1}, use_global_device_ids=true | all-gather | bytes 983040 | tf_op jit(solution)/shard_map/all_gather | solution.py:167
  38.1 0.5 copy.13
  38.6 0.2 pad_bitcast_fusion.q_ref
  38.9 73.5 %shard_map.64 = f32[128,4,8,128]{3,2,1,0:T(8,128)S(1)} custom-call(s32[128]{0:T(128)S(1)} %copy-done, bf16[128,32,128]{2,1,0:T(8,128)(2,1)S(1)} %pad_bitcast_fusion.q_ref, bf16[128,2048,128]{2,1,0:T(8,128)(2,1)} %bitcast.4.k_hbm, bf16[128,2048,128]{2,1,0:T(8,128)(2,1)} %bitcast.5.v_hbm), custom_call_target="tpu_custom_call" | custom-call | tf_op jit(solution)/shard_map/pallas_call | solution.py:141
  112.4 0.4 fusion.2
  112.8 14.3 %pmax.7 = f32[128,4,6]{2,1,0:T(4,128)S(1)} all-reduce(f32[128,4,6]{2,1,0:T(4,128)S(1)} %bitcast.24), channel_id=1, replica_groups=mesh['dp'=1,'kvh'=2,'seq'=4] {'seq'}, use_global_device_ids=true, to_apply=%region_0.1 | all-reduce | flops 3072 | bytes 24576 | tf_op jit(solution)/shard_map/pmax | solution.py:173
  127.1 0.2 fusion.1
  127.3 0.8 slice_multiply_fusion
  128.1 0.0 copy-start.3
  128.1 2.1 copy.15
  130.1 0.0 reduce-scatter.4.cloned.1.call-update
  130.1 0.0 all-reduce.5.cloned.1.call-start
  130.2 0.1 copy.16
  130.3 0.0 copy-done.3
  130.3 0.7 dynamic-slice
  131.0 10.1 %all-reduce.2 = f32[128,4,6]{0,2,1:T(8,128)S(1)} all-reduce(f32[128,4,6]{0,2,1:T(8,128)S(1)} %copy.16), channel_id=3, replica_groups=mesh['dp'=1,'kvh'=2,'seq'=4] {'seq'}, use_global_device_ids=true, to_apply=%region_2.3.clone | all-reduce | flops 3072 | bytes 24576
  141.1 0.6 dynamic-slice_bitcast_fusion
  141.7 11.2 %reduce-scatter.4.cloned.1.call-done = f32[128,1,6,128]{3,0,2,1:T(8,128)} async-done(((f32[128,4,6,128]{3,0,2,1:T(8,128)}), f32[128,1,6,128]{3,0,2,1:T(8,128)}) %reduce-scatter.4.cloned.1.call-update) | async-done | bytes 393232
  152.9 6.9 %convolution_bitcast_fusion = f32[128,6144]{1,0:T(8,128)} fusion(bf16[6,128,6144]{2,1,0:T(8,128)(2,1)} %param.11, f32[128,1,6,128]{3,0,2,1:T(8,128)} %reduce-scatter.4.cloned.1.call-done, f32[128,6]{0,1:T(8,128)S(1)} %dynamic-slice_bitcast_fusion), kind=kOutput, calls=%fused_computation | convolution fusion | flops 1208156160 | bytes 12979200 | tf_op jit(solution)/shard_map/bhk,hkd->bd/dot_general | solution.py:178
  159.8 0.0 copy-start.2
  159.8 0.0 all-reduce.5.cloned.1.call-update
  159.9 58.2 %all-reduce.5.cloned.1.call-done = f32[128,6144]{1,0:T(8,128)} async-done(((f32[128,6144]{1,0:T(8,128)}), f32[128,6144]{1,0:T(8,128)}) %all-reduce.5.cloned.1.call-update) | async-done | bytes 3145744 | tf_op jit(solution)/shard_map/psum | solution.py:179
  218.1 0.0 copy-done.2
  218.1 3.3 %add_convert_fusion = bf16[128,6144]{1,0:T(8,128)(2,1)} fusion(f32[128,6144]{1,0:T(8,128)} %all-reduce.5.cloned.1.call-done, bf16[128,6144]{1,0:T(8,128)(2,1)S(1)} %copy-done.2), kind=kLoop, calls=%fused_computation.1 | loop fusion | flops 2359296 | bytes 6291456 | tf_op jit(solution)/shard_map/convert_element_type | solution.py:180
  (3 shorter events, 0.0 us)
Async XLA Ops:
  6.5 146.4 %reduce-scatter.4.cloned.1.call-start = ((), (), s32[]{:S(2)}) async-start(), calls=%async_computation.2 | async-start | bytes 1966080
  6.5 12.9 %copy-start = (s32[128]{0:T(128)S(1)}, s32[128]{0:T(128)}, u32[]{:S(2)}) copy-start(s32[128]{0:T(128)} %lens_ref.1) | copy-start | bytes 1540
  6.6 12.8 %copy-start.1 = (bf16[128,6144]{1,0:T(8,128)(2,1)S(1)}, bf16[128,6144]{1,0:T(8,128)(2,1)}, u32[]{:S(2)}) copy-start(bf16[128,6144]{1,0:T(8,128)(2,1)} %param.6) | copy-start | bytes 4718596
  128.1 2.3 copy-start.3
  130.1 87.9 %all-reduce.5.cloned.1.call-start = ((), (), s32[]{:S(2)}) async-start(), calls=%async_computation.1 | async-start | bytes 6291456 | tf_op jit(solution)/shard_map/psum | solution.py:179
  159.8 58.2 %copy-start.2 = (bf16[128,6144]{1,0:T(8,128)(2,1)S(1)}, bf16[128,6144]{1,0:T(8,128)(2,1)}, u32[]{:S(2)}) copy-start(bf16[128,6144]{1,0:T(8,128)(2,1)} %param.6) | copy-start | bytes 4718596
Sparse Core Ops, SparseCore 0:
  130.3 22.5 reduce-scatter.3
  160.0 58.0 all-reduce.4

commit v2 on v1

v2 whole, which is shorter than its diff:
```python
import functools

import jax
import jax.numpy as jnp
from jax import lax
from jax.experimental import pallas as pl
from jax.experimental.pallas import tpu as pltpu
from jax.sharding import PartitionSpec as P

ROPE_THETA = 500000.0
HEAD_DIM = 128
NEG = -3.3e38
FLOOR = -3.0e38
LOG2E = 1.4426950408889634
SCALE2 = HEAD_DIM ** -0.5 * LOG2E
SLOTS = 16
UNROLL = 4
Q_ROWS = 32
PART_ROWS = 16
Q_DEPTH = 512
MESH = pl.DeviceIdType.MESH


def rope_tables(seq_lens):
    half_dim = HEAD_DIM // 2
    inv_freq = jnp.power(ROPE_THETA, -jnp.arange(half_dim, dtype=jnp.float32) * (2.0 / HEAD_DIM))
    angle = (seq_lens - 1).astype(jnp.float32)[:, None] * inv_freq[None, :]
    cosine, sine = jnp.cos(angle), jnp.sin(angle)
    return jnp.concatenate([cosine, cosine], -1), jnp.concatenate([-sine, sine], -1)


def head_lanes(width):
    lane = lax.broadcasted_iota(jnp.int32, (8, width), 1)
    return lane, [lane % 4 == n for n in range(4)]


def pick(masks, parts):
    return jnp.where(masks[0], parts[0], jnp.where(masks[1], parts[1], jnp.where(masks[2], parts[2], parts[3])))


def score_row(q32, k_at, limit, s_at, top_at):
    tiles = k_at.shape[0] // 512
    zero = jnp.zeros_like(q32)
    q_diag = jnp.concatenate([jnp.concatenate([q32, zero], 1), jnp.concatenate([zero, q32], 1)], 0)
    lane, masks = head_lanes(256)
    top = None
    for j in range(tiles):
        keys = jnp.concatenate([k_at[pl.ds(512 * j, 256), :], k_at[pl.ds(512 * j + 256, 256), :]], 1)
        s = lax.dot_general(q_diag, keys, (((1,), (1,)), ((), ())), preferred_element_type=jnp.float32)
        for h in range(2):
            mine = pick(masks, [s[32 * h + 8 * n:32 * h + 8 * n + 8] for n in range(4)])
            mine = jnp.where(lane < limit - (512 * j + 256 * h), mine, NEG)
            s_at[:, pl.ds(512 * j + 256 * h, 256)] = mine
            top = mine if top is None else jnp.maximum(top, mine)
    top_at[...] = jnp.maximum(top[:, :128], top[:, 128:])


def weight_row(s_at, top_at, p_at, stat_at):
    tiles = s_at.shape[1] // 512
    _, masks = head_lanes(256)
    _, half = head_lanes(128)
    top = top_at[...]
    tops = [jnp.maximum(jnp.max(jnp.where(half[n], top, NEG), axis=1, keepdims=True), FLOOR) * SCALE2 for n in range(4)]
    shift = pick(half, tops)
    shift = jnp.concatenate([shift, shift], 1)
    total = None
    for j in range(tiles):
        rows = []
        for h in range(2):
            w = jnp.exp2(s_at[:, pl.ds(512 * j + 256 * h, 256)] * SCALE2 - shift)
            total = w if total is None else total + w
            rows += [jnp.where(masks[n], w, 0.0) for n in range(4)]
        p_at[j] = jnp.concatenate(rows, 0).astype(jnp.bfloat16)
    total = total[:, :128] + total[:, 128:]
    row = lax.broadcasted_iota(jnp.int32, (8, 128), 0)
    lane128 = lax.broadcasted_iota(jnp.int32, (8, 128), 1)
    diagonal = row == lane128
    for n in range(4):
        sums = jnp.sum(jnp.where(half[n], total, 0.0), axis=1, keepdims=True)
        top_row = jnp.sum(jnp.where(diagonal, tops[n], 0.0), axis=0, keepdims=True)
        sum_row = jnp.sum(jnp.where(diagonal, sums, 0.0), axis=0, keepdims=True)
        stat_at[n] = jnp.where(row == 6, top_row, sum_row)


def value_row(p_at, v_at, stat_at, out, r):
    tiles = v_at.shape[0] // 512
    acc = None
    for j in range(tiles):
        values = jnp.concatenate([v_at[pl.ds(512 * j, 256), :], v_at[pl.ds(512 * j + 256, 256), :]], 1)
        o = jnp.dot(p_at[j], values, preferred_element_type=jnp.float32)
        acc = o if acc is None else acc + o
    row = lax.broadcasted_iota(jnp.int32, (8, 128), 0)
    for n in range(4):
        o = acc[8 * n:8 * n + 8, :128] + acc[32 + 8 * n:40 + 8 * n, 128:]
        out[n, r] = jnp.where(row < 6, o, stat_at[n])


def add_up(parts):
    return functools.reduce(lambda a, b: a + b, parts)


def merge_rows(parts):
    maxima = [p[:, 6:7, :] for p in parts]
    top = functools.reduce(jnp.maximum, maxima)
    scale = [jnp.exp2(m - top) for m in maxima]
    total = add_up([p[:, 7:8, :] * e for p, e in zip(parts, scale)])
    shape = parts[0].shape
    diagonal = lax.broadcasted_iota(jnp.int32, shape, 1) == lax.broadcasted_iota(jnp.int32, shape, 2)
    factors = [jnp.sum(jnp.where(diagonal, jnp.broadcast_to(e / total, shape), 0.0), axis=2, keepdims=True) for e in scale]
    return add_up([p * f for p, f in zip(parts, factors)])


def decode_kernel(lens_ref, cos_ref, sin_ref, x_hbm, wq_hbm, k_hbm, v_hbm, wo_hbm, out_hbm,
                  x_buf, wq_buf, wo_buf, k_buf, v_buf, q_acc, q_rows, q_all, s_buf, top_buf, p_buf, stat_buf,
                  part, part_in, attn_rows, attn_buf, y_send, y_own, r1, r2, r3, out_buf,
                  x_sem, wq_sem, wo_sem, k_sem, v_sem, q_ssem, q_rsem, part_ssem, part_rsem,
                  y1_ssem, y1_rsem, y2_ssem, y2_rsem, y3_ssem, y3_rsem, ag_ssem, ag_rsem, out_sem):
    rows, model = x_buf.shape
    depth = k_buf.shape[1]
    width = y_own.shape[2]
    groups = rows // UNROLL
    dp, y, s = lax.axis_index('dp'), lax.axis_index('kvh'), lax.axis_index('seq')
    c, x = lax.rem(s, 2), lax.div(s, 2)
    base = s * depth
    seq_peers = [s + 1 - 2 * c, lax.rem(s + 2, 4), 3 - s]
    partner = (dp, y, s + 1 - 2 * c)
    first_axis = (dp, y + c * (1 - 2 * y), lax.rem(s + 2 * (1 - c), 4))
    second_axis = (dp, y + (1 - c) * (1 - 2 * y), lax.rem(s + 2 * c, 4))
    am, bm = x + c * (y - x), y + c * (x - y)

    def remote(src, dst, ssem, rsem, device):
        return pltpu.make_async_remote_copy(src_ref=src, dst_ref=dst, send_sem=ssem, recv_sem=rsem,
                                            device_id=device, device_id_type=MESH)

    barrier = pltpu.get_barrier_semaphore()
    for device in [(dp, y, p) for p in seq_peers] + [(dp, 1 - y, s)]:
        pl.semaphore_signal(barrier, inc=1, device_id=device, device_id_type=MESH)

    x_copy = pltpu.make_async_copy(x_hbm, x_buf, x_sem)
    x_copy.start()

    def wq_copy(i):
        return pltpu.make_async_copy(wq_hbm.at[:, pl.ds(i * Q_DEPTH, Q_DEPTH), :], wq_buf.at[i], wq_sem.at[i])

    def wo_copy(i):
        return pltpu.make_async_copy(wo_hbm.at[:, pl.ds(pl.multiple_of(i * width, 128), width)], wo_buf.at[i], wo_sem.at[i])

    def k_copy(r):
        slot = lax.rem(r, SLOTS)
        return pltpu.make_async_copy(k_hbm.at[r], k_buf.at[slot], k_sem.at[slot])

    def v_copy(r):
        slot = lax.rem(r, SLOTS)
        return pltpu.make_async_copy(v_hbm.at[r], v_buf.at[slot], v_sem.at[slot])

    def each(n, f, first=0):
        def step(i, carry):
            f(i)
            return carry
        lax.fori_loop(first, n, step, 0)

    q_steps = model // Q_DEPTH
    each(q_steps, lambda i: wq_copy(i).start())

    def prime(r):
        k_copy(r).start()
        v_copy(r).start()
    each(SLOTS, prime)
    each(8, lambda i: wo_copy(i).start())

    q_acc[...] = jnp.zeros_like(q_acc)
    q_rows[...] = jnp.zeros_like(q_rows)
    x_copy.wait()

    def project(i):
        wq_copy(i).wait()
        weights = jnp.concatenate([wq_buf[i, g] for g in range(6)], 1)
        cols = pl.ds(pl.multiple_of(i * Q_DEPTH, 128), Q_DEPTH)
        q_acc[...] += jnp.dot(x_buf[:, cols], weights, preferred_element_type=jnp.float32)
    each(q_steps, project)
    for g in range(6):
        q = q_acc[:, g * HEAD_DIM:(g + 1) * HEAD_DIM]
        q = q * cos_ref[...] + pltpu.roll(q, HEAD_DIM // 2, 1) * sin_ref[...]
        q_rows[pl.ds(g, rows, stride=8), :] = q
    q_all[s] = q_rows[...].reshape(rows, 8, HEAD_DIM).astype(jnp.bfloat16)
    pl.semaphore_wait(barrier, 4)

    def q_send(d, i):
        piece = q_all.at[s, pl.ds(i * Q_ROWS, Q_ROWS)]
        return remote(piece, piece, q_ssem.at[d, i], q_rsem.at[d, i], (dp, y, seq_peers[d]))

    def q_chunk(i):
        for d in range(3):
            q_send(d, i).start()
    each(rows // Q_ROWS, q_chunk)

    def part_send(d, i):
        chunk = pl.ds(i * PART_ROWS, PART_ROWS)
        return remote(part.at[seq_peers[d], chunk], part_in.at[d, chunk], part_ssem.at[d, i], part_rsem.at[d, i],
                      (dp, y, seq_peers[d]))

    def merge(i):
        for d in range(3):
            part_send(d, i).wait_recv()
        for h in range(PART_ROWS // 8):
            chunk = pl.ds(i * PART_ROWS + 8 * h, 8)
            merged = merge_rows([part[s, chunk]] + [part_in[d, chunk] for d in range(3)])
            attn_rows[pl.ds(pl.multiple_of((i * PART_ROWS + 8 * h) * 8, 64), 64), :] = merged.reshape(64, HEAD_DIM)

    def attend(i, stages):
        parity = lax.rem(i, 2)
        ahead = i * UNROLL
        back = (i - 2) * UNROLL
        if 'a' in stages:
            @pl.when(lax.rem(ahead, Q_ROWS) == 0)
            def _():
                for d in range(3):
                    q_send(d, lax.div(ahead, Q_ROWS)).wait_recv()
            for u in range(UNROLL):
                k_copy(ahead + u).wait()
        if 'c' in stages:
            for u in range(UNROLL):
                v_copy(back + u).wait()
        if 'a' in stages:
            for u in range(UNROLL):
                r = ahead + u
                q32 = jnp.concatenate([q_all[n, r] for n in range(4)], 0)
                score_row(q32, k_buf.at[lax.rem(r, SLOTS)], lens_ref[r] * 4 - base, s_buf.at[parity, u], top_buf.at[parity, u])
        if 'c' in stages:
            for u in range(UNROLL):
                r = back + u
                value_row(p_buf.at[parity, u], v_buf.at[lax.rem(r, SLOTS)], stat_buf.at[parity, u], part, r)
        if 'b' in stages:
            for u in range(UNROLL):
                weight_row(s_buf.at[1 - parity, u], top_buf.at[1 - parity, u], p_buf.at[1 - parity, u], stat_buf.at[1 - parity, u])
        if 'a' in stages:
            @pl.when(ahead + SLOTS < rows)
            def _():
                for u in range(UNROLL):
                    k_copy(ahead + u + SLOTS).start()
        if 'c' in stages:
            @pl.when(back + SLOTS < rows)
            def _():
                for u in range(UNROLL):
                    v_copy(back + u + SLOTS).start()

            @pl.when(lax.rem(back + UNROLL, PART_ROWS) == 0)
            def _():
                chunk = lax.div(back, PART_ROWS)
                for d in range(3):
                    part_send(d, chunk).start()

                @pl.when(chunk > 0)
                def _():
                    merge(chunk - 1)
    attend(0, 'a')
    attend(1, 'ab')
    each(groups, lambda i: attend(i, 'abc'), 2)
    attend(groups, 'bc')
    attend(groups + 1, 'c')
    merge(rows // PART_ROWS - 1)

    for g in range(6):
        attn_buf[:, g * HEAD_DIM:(g + 1) * HEAD_DIM] = attn_rows[pl.ds(g, rows, stride=8), :].astype(jnp.bfloat16)
    each(8, lambda i: wo_copy(i).wait())

    def block(b):
        return jnp.dot(attn_buf[...], wo_buf[b], preferred_element_type=jnp.float32)

    def to_partner(j):
        return remote(y_send.at[j], r1.at[j], y1_ssem.at[j], y1_rsem.at[j], partner)

    def partner_half(j):
        y_send[j] = block(4 * (1 - c) + j)
        to_partner(j).start()
    each(4, partner_half)

    def to_first(k):
        return remote(y_own.at[k], r2.at[k], y2_ssem.at[k], y2_rsem.at[k], first_axis)

    def own_half(k):
        o = 2 * ((1 - am) + lax.div(k, 2) * (2 * am - 1)) + (1 - bm) + lax.rem(k, 2) * (2 * bm - 1)
        mine = block(4 * c + o)
        to_partner(o).wait_recv()
        y_own[k] = mine + r1[o]

        @pl.when(k < 2)
        def _():
            to_first(k).start()
    each(4, own_half)

    to_first(0).wait_recv()
    y_own[2] = y_own[2] + r2[0]
    to_second = remote(y_own.at[2], r3, y3_ssem, y3_rsem, second_axis)
    to_second.start()
    to_first(1).wait_recv()
    y_own[3] = y_own[3] + r2[1]
    to_second.wait_recv()

    def block_id(fa, fb):
        a = am if fa == 0 else 1 - am
        b = bm if fb == 0 else 1 - bm
        return 4 * c + 2 * a + b
    mine = block_id(0, 0)
    x_cols = x_buf[:, pl.ds(pl.multiple_of(mine * width, 128), width)].astype(jnp.float32)
    out_buf[mine] = (x_cols + (y_own[3] + r3[...])).astype(jnp.bfloat16)

    def gather(i, b, device):
        return remote(out_buf.at[b], out_buf.at[b], ag_ssem.at[i], ag_rsem.at[i], device)

    def store(b):
        return pltpu.make_async_copy(out_buf.at[b], out_hbm.at[:, pl.ds(pl.multiple_of(b * width, 128), width)], out_sem.at[b])
    blocks = [block_id(0, 0), block_id(0, 1), block_id(1, 0), block_id(1, 1)]
    theirs = [4 - 4 * c + j for j in range(4)]
    sends = [gather(0, blocks[0], second_axis), gather(1, blocks[0], first_axis), gather(3, blocks[0], partner)]
    for send in sends:
        send.start()
    store(blocks[0]).start()

    def pass_on(i, b, targets):
        gather(i, b, partner).wait_recv()
        for j, device in targets:
            send = gather(j, b, device)
            send.start()
            sends.append(send)
        store(b).start()
    pass_on(0, blocks[1], [(2, first_axis), (4, partner)])
    pass_on(1, blocks[2], [(5, partner)])
    pass_on(2, blocks[3], [(6, partner)])
    pc = 1 - c
    pam, pbm = x + pc * (y - x), y + pc * (x - y)
    partner_blocks = [4 * pc + 2 * pam + pbm, 4 * pc + 2 * pam + 1 - pbm, 4 * pc + 2 * (1 - pam) + pbm, 4 * pc + 2 * (1 - pam) + 1 - pbm]
    for i, b in zip((3, 4, 5, 6), partner_blocks):
        gather(i, b, partner).wait_recv()
        store(b).start()

    for d in range(3):
        each(rows // Q_ROWS, lambda i: q_send(d, i).wait_send())
        each(rows // PART_ROWS, lambda i: part_send(d, i).wait_send())
    each(4, lambda j: to_partner(j).wait_send())
    each(2, lambda k: to_first(k).wait_send())
    to_second.wait_send()
    for send in sends:
        send.wait_send()
    each(8, lambda b: store(b).wait())


def decode(seq_lens, x_hidden, k_loc, v_loc, wq_loc, wo_loc):
    rows, depth = k_loc.shape[0], k_loc.shape[1]
    model = x_hidden.shape[1]
    width = model // 8
    cosine, sine = rope_tables(seq_lens)
    bf16, f32 = jnp.bfloat16, jnp.float32
    dma = pltpu.SemaphoreType.DMA
    q_chunks, part_chunks = rows // Q_ROWS, rows // PART_ROWS
    vmem, hbm = pl.BlockSpec(memory_space=pltpu.VMEM), pl.BlockSpec(memory_space=pl.ANY)
    return pl.pallas_call(
        decode_kernel,
        out_shape=jax.ShapeDtypeStruct((rows, model), bf16),
        in_specs=[pl.BlockSpec(memory_space=pltpu.SMEM), vmem, vmem, hbm, hbm, hbm, hbm, hbm],
        out_specs=hbm,
        scratch_shapes=[
            pltpu.VMEM((rows, model), bf16),
            pltpu.VMEM((model // Q_DEPTH, 6, Q_DEPTH, HEAD_DIM), bf16),
            pltpu.VMEM((8, 6 * HEAD_DIM, width), bf16),
            pltpu.VMEM((SLOTS, depth, HEAD_DIM), bf16),
            pltpu.VMEM((SLOTS, depth, HEAD_DIM), bf16),
            pltpu.VMEM((rows, 6 * HEAD_DIM), f32),
            pltpu.VMEM((rows * 8, HEAD_DIM), f32),
            pltpu.VMEM((4, rows, 8, HEAD_DIM), bf16),
            pltpu.VMEM((2, UNROLL, 8, depth), f32),
            pltpu.VMEM((2, UNROLL, 8, HEAD_DIM), f32),
            pltpu.VMEM((2, UNROLL, depth // 512, 64, 256), bf16),
            pltpu.VMEM((2, UNROLL, 4, 8, HEAD_DIM), f32),
            pltpu.VMEM((4, rows, 8, HEAD_DIM), f32),
            pltpu.VMEM((3, rows, 8, HEAD_DIM), f32),
            pltpu.VMEM((rows * 8, HEAD_DIM), f32),
            pltpu.VMEM((rows, 6 * HEAD_DIM), bf16),
            pltpu.VMEM((4, rows, width), f32),
            pltpu.VMEM((4, rows, width), f32),
            pltpu.VMEM((4, rows, width), f32),
            pltpu.VMEM((2, rows, width), f32),
            pltpu.VMEM((rows, width), f32),
            pltpu.VMEM((8, rows, width), bf16),
            dma, dma((model // Q_DEPTH,)), dma((8,)), dma((SLOTS,)), dma((SLOTS,)),
            dma((3, q_chunks)), dma((3, q_chunks)), dma((3, part_chunks)), dma((3, part_chunks)),
            dma((4,)), dma((4,)), dma((2,)), dma((2,)), dma, dma, dma((7,)), dma((7,)), dma((8,)),
        ],
        compiler_params=pltpu.CompilerParams(vmem_limit_bytes=62 * 2 ** 20, collective_id=0, has_side_effects=True),
    )(seq_lens, cosine, sine, x_hidden, wq_loc, k_loc, v_loc, wo_loc)


def solution(mesh):
    def local_step(x_hidden, seq_lens, k_loc, v_loc, wq_loc, wo_loc):
        rows, t_dev, kv_loc, head_dim = k_loc.shape
        return decode(seq_lens, x_hidden, k_loc.reshape(rows, t_dev * kv_loc, head_dim),
                      v_loc.reshape(rows, t_dev * kv_loc, head_dim), wq_loc.transpose(1, 0, 2),
                      wo_loc.reshape(-1, wo_loc.shape[2]))

    return jax.shard_map(
        local_step,
        mesh=mesh,
        in_specs=(P('dp', None), P('dp'), P('dp', 'seq', 'kvh', None), P('dp', 'seq', 'kvh', None),
                  P(None, ('kvh', 'seq'), None), P(('kvh', 'seq'), None, None)),
        out_specs=P('dp', None),
        check_vma=False)
```

time: 229 us -> 94.9 us (0.41)
  waiting for transfers between devices: 69.4 us -> 0 us
  blocking collectives: 37.4 us -> 0 us
  Pallas kernels: 73.5 us -> 90.1 us
  local copies, waits for them, and re-layouts: 17.6 us -> 2.69 us
  between operations: 13.5 us -> 0.02 us
  matrix products: 12.1 us -> 0 us
  other arithmetic: 4.54 us -> 1.72 us
    psum x1 -> x0, waiting for transfers between devices: 58.2 us -> none  [local_step(): y_sum = lax.psum(y_part, ('kvh', 'seq'))]
    pallas_call x1, Pallas kernels: 73.5 us -> 90.1 us  [decode(): pl.pallas_call(decode_kernel, out_shape=jax.ShapeDtypeStruct((rows, model...]
    pmax x1 -> x0, blocking collectives: 14.3 us -> none  [local_step(): global_max = lax.pmax(local_max, 'seq')]
    all_gather x1 -> x0, blocking collectives: 13 us -> none  [local_step(): lax.all_gather(q_own, 'seq', axis=1, tiled=True)]
    unnamed x3 -> x0, waiting for transfers between devices: 11.2 us -> none
    unnamed x10 -> x1, local copies, waits for them, and re-layouts: 13.5 us -> 2.69 us
    unnamed x1 -> x0, blocking collectives: 10.1 us -> none
    dot_general x1 -> x0, matrix products: 6.93 us -> none  [local_step(): jnp.einsum('bhk,hkd->bd', attn, wo_loc, preferred_element_type=jnp.float32)]
  transfers between devices with their start and end apart: 2 -> 0, of which waited for: 2 -> 0; matrix products, arithmetic and copies ran while one was open for 1% -> 0% of each run, Pallas kernels for 0% -> 0%
where the time goes in v2:
time: 94.9 us; the launch traced here: 94.5 us
  Pallas kernels  90.1 us (95%)
  local copies, waits for them, and re-layouts  2.69 us (3%)
  other arithmetic  1.72 us (2%)
    pallas_call x1, Pallas kernels, decode(): pl.pallas_call(decode_kernel, out_shape=jax.ShapeDtypeStruct((rows, model...  90.1 us
    unnamed x1, local copies, waits for them, and re-layouts  2.69 us

profile of v2, /device:TPU:0, one launch (start us, length us, event | category | flops | bytes accessed | tf_op | source)
XLA Modules:
  0.0 94.5 jit_solution(9862420199267767100)
XLA Ops:
  0.0 0.7 add_convert_fusion
  0.7 0.3 fusion
  1.0 0.7 pad_maximum_fusion
  1.7 90.1 %shard_map.64 = bf16[128,6144]{1,0:T(8,128)(2,1)} custom-call(s32[128]{0:T(128)} %lens_ref.1, f32[128,128]{1,0:T(8,128)} %get-tuple-element.8.cos_ref, f32[128,128]{1,0:T(8,128)} %get-tuple-element.9.sin_ref, bf16[128,6144]{1,0:T(8,128)(2,1)} %x_hbm.1, bf16[6,6144,128]{2,1,0:T(8,128)(2,1)} %bitcast.4, bf16[128,2048,128]{2,1,0:T(8,128)(2,1)} %bitcast.1.k_hbm, ...), custom_call_target="tpu_custom_call" | custom-call | tf_op jit(solution)/shard_map/pallas_call | solution.py:357
  91.9 2.7 %copy.8 = bf16[128,6144]{1,0:T(8,128)(2,1)} copy(bf16[128,6144]{1,0:T(8,128)(2,1)} %shard_map.64) | data formatting | bytes 3145728
  (1 shorter events, 0.0 us)

commit v3 on v2

--- a/solution.py
+++ b/solution.py
@@ -2,6 +2,7 @@
 
 import jax
 import jax.numpy as jnp
+import numpy as np
 from jax import lax
 from jax.experimental import pallas as pl
 from jax.experimental.pallas import tpu as pltpu
@@ -16,17 +17,14 @@
 SLOTS = 16
 UNROLL = 4
 Q_ROWS = 32
-PART_ROWS = 16
+PART_ROWS = 8
+PART_LAG = 2
+ROW_GROUPS = ((0, 48), (48, 48), (96, 32))
 Q_DEPTH = 512
+LOOP_STEPS = ((17, 0, 'project'), (19, 0, 'first'), (23, 0, 'second'), (27, 0, 'finish'), (29, 1, 'project'), (31, 1, 'first'))
+TAIL_STEPS = ((2, 'project'), (0, 'relay'), (1, 'second'), (2, 'first'), (0, 'relay_last'), (1, 'finish'), (2, 'second'), (2, 'finish'),
+              (1, 'relay'), (1, 'relay_last'), (0, 'collect'), (2, 'relay'), (2, 'relay_last'), (1, 'collect'), (2, 'collect'))
 MESH = pl.DeviceIdType.MESH
-
-
-def rope_tables(seq_lens):
-    half_dim = HEAD_DIM // 2
-    inv_freq = jnp.power(ROPE_THETA, -jnp.arange(half_dim, dtype=jnp.float32) * (2.0 / HEAD_DIM))
-    angle = (seq_lens - 1).astype(jnp.float32)[:, None] * inv_freq[None, :]
-    cosine, sine = jnp.cos(angle), jnp.sin(angle)
-    return jnp.concatenate([cosine, cosine], -1), jnp.concatenate([-sine, sine], -1)
 
 
 def head_lanes(width):
@@ -110,10 +108,10 @@
     return add_up([p * f for p, f in zip(parts, factors)])
 
 
-def decode_kernel(lens_ref, cos_ref, sin_ref, x_hbm, wq_hbm, k_hbm, v_hbm, wo_hbm, out_hbm,
-                  x_buf, wq_buf, wo_buf, k_buf, v_buf, q_acc, q_rows, q_all, s_buf, top_buf, p_buf, stat_buf,
+def decode_kernel(lens_ref, freq_hbm, x_hbm, wq_hbm, k_hbm, v_hbm, wo_hbm, out_hbm,
+                  freq_buf, pos_buf, cos_buf, sin_buf, x_buf, wq_buf, wo_buf, k_buf, v_buf, q_acc, q_rows, q_all, s_buf, top_buf, p_buf, stat_buf,
                   part, part_in, attn_rows, attn_buf, y_send, y_own, r1, r2, r3, out_buf,
-                  x_sem, wq_sem, wo_sem, k_sem, v_sem, q_ssem, q_rsem, part_ssem, part_rsem,
+                  freq_sem, x_sem, wq_sem, wo_sem, k_sem, v_sem, q_ssem, q_rsem, part_ssem, part_rsem,
                   y1_ssem, y1_rsem, y2_ssem, y2_rsem, y3_ssem, y3_rsem, ag_ssem, ag_rsem, out_sem):
     rows, model = x_buf.shape
     depth = k_buf.shape[1]
@@ -124,9 +122,6 @@
     base = s * depth
     seq_peers = [s + 1 - 2 * c, lax.rem(s + 2, 4), 3 - s]
     partner = (dp, y, s + 1 - 2 * c)
-    first_axis = (dp, y + c * (1 - 2 * y), lax.rem(s + 2 * (1 - c), 4))
-    second_axis = (dp, y + (1 - c) * (1 - 2 * y), lax.rem(s + 2 * c, 4))
-    am, bm = x + c * (y - x), y + c * (x - y)
 
     def remote(src, dst, ssem, rsem, device):
         return pltpu.make_async_remote_copy(src_ref=src, dst_ref=dst, send_sem=ssem, recv_sem=rsem,
@@ -136,6 +131,8 @@
     for device in [(dp, y, p) for p in seq_peers] + [(dp, 1 - y, s)]:
         pl.semaphore_signal(barrier, inc=1, device_id=device, device_id_type=MESH)
 
+    freq_copy = pltpu.make_async_copy(freq_hbm, freq_buf, freq_sem)
+    freq_copy.start()
     x_copy = pltpu.make_async_copy(x_hbm, x_buf, x_sem)
     x_copy.start()
 
@@ -170,6 +167,18 @@
 
     q_acc[...] = jnp.zeros_like(q_acc)
     q_rows[...] = jnp.zeros_like(q_rows)
+
+    def position(i):
+        for u in range(8):
+            r = 8 * i + u
+            pos_buf[pl.ds(r, 1), :] = jnp.broadcast_to(lens_ref[r] - 1, (1, HEAD_DIM)).astype(jnp.float32)
+    each(rows // 8, position)
+    freq_copy.wait()
+    angle = pos_buf[...] * freq_buf[...]
+    q_sin = jnp.sin(angle)
+    lane = lax.broadcasted_iota(jnp.int32, angle.shape, 1)
+    cos_buf[...] = jnp.cos(angle)
+    sin_buf[...] = jnp.where(lane < HEAD_DIM // 2, -q_sin, q_sin)
     x_copy.wait()
 
     def project(i):
@@ -180,7 +189,7 @@
     each(q_steps, project)
     for g in range(6):
         q = q_acc[:, g * HEAD_DIM:(g + 1) * HEAD_DIM]
-        q = q * cos_ref[...] + pltpu.roll(q, HEAD_DIM // 2, 1) * sin_ref[...]
+        q = q * cos_buf[...] + pltpu.roll(q, HEAD_DIM // 2, 1) * sin_buf[...]
         q_rows[pl.ds(g, rows, stride=8), :] = q
     q_all[s] = q_rows[...].reshape(rows, 8, HEAD_DIM).astype(jnp.bfloat16)
     pl.semaphore_wait(barrier, 4)
@@ -202,10 +211,10 @@
     def merge(i):
         for d in range(3):
             part_send(d, i).wait_recv()
-        for h in range(PART_ROWS // 8):
-            chunk = pl.ds(i * PART_ROWS + 8 * h, 8)
-            merged = merge_rows([part[s, chunk]] + [part_in[d, chunk] for d in range(3)])
-            attn_rows[pl.ds(pl.multiple_of((i * PART_ROWS + 8 * h) * 8, 64), 64), :] = merged.reshape(64, HEAD_DIM)
+        chunk = pl.ds(i * PART_ROWS, PART_ROWS)
+        merged = merge_rows([part[s, chunk]] + [part_in[d, chunk] for d in range(3)])
+        span = PART_ROWS * 8
+        attn_rows[pl.ds(pl.multiple_of(i * span, span), span), :] = merged.reshape(span, HEAD_DIM)
 
     def attend(i, stages):
         parity = lax.rem(i, 2)
@@ -250,116 +259,168 @@
                 for d in range(3):
                     part_send(d, chunk).start()
 
-                @pl.when(chunk > 0)
+                @pl.when(chunk >= PART_LAG)
                 def _():
-                    merge(chunk - 1)
+                    merge(chunk - PART_LAG)
+
+    def reduction(g, first_row, count, early):
+        span = pl.ds(first_row, count)
+        cc = 1 if early else c
+        first_axis = (dp, y + cc * (1 - 2 * y), lax.rem(s + 2 * (1 - cc), 4))
+        second_axis = (dp, y + (1 - cc) * (1 - 2 * y), lax.rem(s + 2 * cc, 4))
+        am, bm = x + cc * (y - x), y + cc * (x - y)
+        sends = []
+
+        def block(b):
+            return jnp.dot(attn_buf[span, :], wo_buf[b], preferred_element_type=jnp.float32)
+
+        def to_partner(j):
+            return remote(y_send.at[j, span], r1.at[j, span], y1_ssem.at[g, j], y1_rsem.at[g, j], partner)
+
+        def offset(k):
+            fa, fb = 1 - k // 2, 1 - k % 2
+            return 2 * (am + fa * (1 - 2 * am)) + bm + fb * (1 - 2 * bm)
+
+        def to_first(k):
+            return remote(y_own.at[k, span], r2.at[k, span], y2_ssem.at[g, k], y2_rsem.at[g, k], first_axis)
+
+        def to_second():
+            return remote(y_own.at[2, span], r3.at[span], y3_ssem.at[g], y3_rsem.at[g], second_axis)
+
+        def gather(i, b, device):
+            return remote(out_buf.at[b, span], out_buf.at[b, span], ag_ssem.at[g, i], ag_rsem.at[g, i], device)
+
+        def store(b):
+            return pltpu.make_async_copy(out_buf.at[b, span], out_hbm.at[span, pl.ds(pl.multiple_of(b * width, 128), width)],
+                                         out_sem.at[g, b])
+        blocks = [4 * c + offset(3 - i) for i in range(4)]
+
+        def project():
+            for h in range(6):
+                rows_of_head = attn_rows[pl.ds(8 * first_row + h, count, stride=8), :]
+                attn_buf[span, h * HEAD_DIM:(h + 1) * HEAD_DIM] = rows_of_head.astype(jnp.bfloat16)
+
+            def partner_half(j):
+                ahead = [block(4 * (1 - c) + 2 * j + u) for u in range(2)]
+                for u in range(2):
+                    y_send[2 * j + u, span, :] = ahead[u]
+                    to_partner(2 * j + u).start()
+            each(2, partner_half)
+
+            def own_half(k):
+                fa = 1 - k
+                base_block = 4 * c + 2 * (am + fa * (1 - 2 * am))
+                ahead = [block(base_block + bm + (1 - u) * (1 - 2 * bm)) for u in range(2)]
+                for u in range(2):
+                    y_own[2 * k + u, span, :] = ahead[u]
+            each(2, own_half)
+
+        def first():
+            for k in range(4):
+                o = offset(k)
+                to_partner(o).wait_recv()
+                y_own[k, span, :] = y_own[k, span, :] + r1[o, span, :]
+                if k < 2:
+                    to_first(k).start()
+
+        def second():
+            to_first(0).wait_recv()
+            y_own[2, span, :] = y_own[2, span, :] + r2[0, span, :]
+            to_second().start()
+
+        def finish():
+            to_first(1).wait_recv()
+            y_own[3, span, :] = y_own[3, span, :] + r2[1, span, :]
+            to_second().wait_recv()
+            x_cols = x_buf[span, pl.ds(pl.multiple_of(blocks[0] * width, 128), width)].astype(jnp.float32)
+            out_buf[blocks[0], span, :] = (x_cols + (y_own[3, span, :] + r3[span, :])).astype(jnp.bfloat16)
+            for i, device in ((0, second_axis), (1, first_axis), (3, partner)):
+                sends.append(gather(i, blocks[0], device))
+                sends[-1].start()
+            store(blocks[0]).start()
+
+        def pass_on(i, targets):
+            b = blocks[1 + i]
+            gather(i, b, partner).wait_recv()
+            for j, device in targets:
+                sends.append(gather(j, b, device))
+                sends[-1].start()
+            store(b).start()
+
+        def relay():
+            pass_on(0, [(2, first_axis), (4, partner)])
+            pass_on(1, [(5, partner)])
+
+        def relay_last():
+            pass_on(2, [(6, partner)])
+
+        def collect():
+            pc = 1 - c
+            pcc = 1 if early else pc
+            pam, pbm = x + pcc * (y - x), y + pcc * (x - y)
+            for i in range(4):
+                a = pam if i < 2 else 1 - pam
+                b = 4 * pc + 2 * a + (pbm if i % 2 == 0 else 1 - pbm)
+                gather(3 + i, b, partner).wait_recv()
+                store(b).start()
+
+        def drain():
+            each(4, lambda j: to_partner(j).wait_send())
+            each(2, lambda k: to_first(k).wait_send())
+            to_second().wait_send()
+            for send in sends:
+                send.wait_send()
+            each(8, lambda b: store(b).wait())
+        return dict(project=project, first=first, second=second, finish=finish, relay=relay, relay_last=relay_last,
+                    collect=collect, drain=drain)
+    reductions = [reduction(g, r, n, g + 1 < len(ROW_GROUPS)) for g, (r, n) in enumerate(ROW_GROUPS)]
+
     attend(0, 'a')
     attend(1, 'ab')
-    each(groups, lambda i: attend(i, 'abc'), 2)
+    at = 2
+    for stop, g, name in LOOP_STEPS:
+        if stop + 1 > at:
+            each(stop + 1, lambda i: attend(i, 'abc'), at)
+            at = stop + 1
+        if (g, name) == (0, 'project'):
+            each(8, lambda i: wo_copy(i).wait())
+        reductions[g][name]()
+    each(groups, lambda i: attend(i, 'abc'), at)
     attend(groups, 'bc')
     attend(groups + 1, 'c')
-    merge(rows // PART_ROWS - 1)
-
-    for g in range(6):
-        attn_buf[:, g * HEAD_DIM:(g + 1) * HEAD_DIM] = attn_rows[pl.ds(g, rows, stride=8), :].astype(jnp.bfloat16)
-    each(8, lambda i: wo_copy(i).wait())
-
-    def block(b):
-        return jnp.dot(attn_buf[...], wo_buf[b], preferred_element_type=jnp.float32)
-
-    def to_partner(j):
-        return remote(y_send.at[j], r1.at[j], y1_ssem.at[j], y1_rsem.at[j], partner)
-
-    def partner_half(j):
-        y_send[j] = block(4 * (1 - c) + j)
-        to_partner(j).start()
-    each(4, partner_half)
-
-    def to_first(k):
-        return remote(y_own.at[k], r2.at[k], y2_ssem.at[k], y2_rsem.at[k], first_axis)
-
-    def own_half(k):
-        o = 2 * ((1 - am) + lax.div(k, 2) * (2 * am - 1)) + (1 - bm) + lax.rem(k, 2) * (2 * bm - 1)
-        mine = block(4 * c + o)
-        to_partner(o).wait_recv()
-        y_own[k] = mine + r1[o]
-
-        @pl.when(k < 2)
-        def _():
-            to_first(k).start()
-    each(4, own_half)
-
-    to_first(0).wait_recv()
-    y_own[2] = y_own[2] + r2[0]
-    to_second = remote(y_own.at[2], r3, y3_ssem, y3_rsem, second_axis)
-    to_second.start()
-    to_first(1).wait_recv()
-    y_own[3] = y_own[3] + r2[1]
-    to_second.wait_recv()
-
-    def block_id(fa, fb):
-        a = am if fa == 0 else 1 - am
-        b = bm if fb == 0 else 1 - bm
-        return 4 * c + 2 * a + b
-    mine = block_id(0, 0)
-    x_cols = x_buf[:, pl.ds(pl.multiple_of(mine * width, 128), width)].astype(jnp.float32)
-    out_buf[mine] = (x_cols + (y_own[3] + r3[...])).astype(jnp.bfloat16)
-
-    def gather(i, b, device):
-        return remote(out_buf.at[b], out_buf.at[b], ag_ssem.at[i], ag_rsem.at[i], device)
-
-    def store(b):
-        return pltpu.make_async_copy(out_buf.at[b], out_hbm.at[:, pl.ds(pl.multiple_of(b * width, 128), width)], out_sem.at[b])
-    blocks = [block_id(0, 0), block_id(0, 1), block_id(1, 0), block_id(1, 1)]
-    theirs = [4 - 4 * c + j for j in range(4)]
-    sends = [gather(0, blocks[0], second_axis), gather(1, blocks[0], first_axis), gather(3, blocks[0], partner)]
-    for send in sends:
-        send.start()
-    store(blocks[0]).start()
-
-    def pass_on(i, b, targets):
-        gather(i, b, partner).wait_recv()
-        for j, device in targets:
-            send = gather(j, b, device)
-            send.start()
-            sends.append(send)
-        store(b).start()
-    pass_on(0, blocks[1], [(2, first_axis), (4, partner)])
-    pass_on(1, blocks[2], [(5, partner)])
-    pass_on(2, blocks[3], [(6, partner)])
-    pc = 1 - c
-    pam, pbm = x + pc * (y - x), y + pc * (x - y)
-    partner_blocks = [4 * pc + 2 * pam + pbm, 4 * pc + 2 * pam + 1 - pbm, 4 * pc + 2 * (1 - pam) + pbm, 4 * pc + 2 * (1 - pam) + 1 - pbm]
-    for i, b in zip((3, 4, 5, 6), partner_blocks):
-        gather(i, b, partner).wait_recv()
-        store(b).start()
+    for i in range(PART_LAG):
+        merge(rows // PART_ROWS - PART_LAG + i)
+    for g, name in TAIL_STEPS:
+        reductions[g][name]()
 
     for d in range(3):
         each(rows // Q_ROWS, lambda i: q_send(d, i).wait_send())
         each(rows // PART_ROWS, lambda i: part_send(d, i).wait_send())
-    each(4, lambda j: to_partner(j).wait_send())
-    each(2, lambda k: to_first(k).wait_send())
-    to_second.wait_send()
-    for send in sends:
-        send.wait_send()
-    each(8, lambda b: store(b).wait())
+    for r in reductions:
+        r['drain']()
 
 
 def decode(seq_lens, x_hidden, k_loc, v_loc, wq_loc, wo_loc):
     rows, depth = k_loc.shape[0], k_loc.shape[1]
     model = x_hidden.shape[1]
     width = model // 8
-    cosine, sine = rope_tables(seq_lens)
+    inv_freq = np.power(ROPE_THETA, -np.arange(HEAD_DIM // 2) * (2.0 / HEAD_DIM)).astype(np.float32)
+    inv_freq = jnp.asarray(np.concatenate([inv_freq, inv_freq])[None])
     bf16, f32 = jnp.bfloat16, jnp.float32
     dma = pltpu.SemaphoreType.DMA
     q_chunks, part_chunks = rows // Q_ROWS, rows // PART_ROWS
-    vmem, hbm = pl.BlockSpec(memory_space=pltpu.VMEM), pl.BlockSpec(memory_space=pl.ANY)
+    n = len(ROW_GROUPS)
+    hbm = pl.BlockSpec(memory_space=pl.ANY)
     return pl.pallas_call(
         decode_kernel,
         out_shape=jax.ShapeDtypeStruct((rows, model), bf16),
-        in_specs=[pl.BlockSpec(memory_space=pltpu.SMEM), vmem, vmem, hbm, hbm, hbm, hbm, hbm],
+        in_specs=[pl.BlockSpec(memory_space=pltpu.SMEM), hbm, hbm, hbm, hbm, hbm, hbm],
         out_specs=hbm,
         scratch_shapes=[
+            pltpu.VMEM((1, HEAD_DIM), f32),
+            pltpu.VMEM((rows, HEAD_DIM), f32),
+            pltpu.VMEM((rows, HEAD_DIM), f32),
+            pltpu.VMEM((rows, HEAD_DIM), f32),
             pltpu.VMEM((rows, model), bf16),
             pltpu.VMEM((model // Q_DEPTH, 6, Q_DEPTH, HEAD_DIM), bf16),
             pltpu.VMEM((8, 6 * HEAD_DIM, width), bf16),
@@ -382,12 +443,12 @@
             pltpu.VMEM((2, rows, width), f32),
             pltpu.VMEM((rows, width), f32),
             pltpu.VMEM((8, rows, width), bf16),
-            dma, dma((model // Q_DEPTH,)), dma((8,)), dma((SLOTS,)), dma((SLOTS,)),
+            dma, dma, dma((model // Q_DEPTH,)), dma((8,)), dma((SLOTS,)), dma((SLOTS,)),
             dma((3, q_chunks)), dma((3, q_chunks)), dma((3, part_chunks)), dma((3, part_chunks)),
-            dma((4,)), dma((4,)), dma((2,)), dma((2,)), dma, dma, dma((7,)), dma((7,)), dma((8,)),
+            dma((n, 4)), dma((n, 4)), dma((n, 2)), dma((n, 2)), dma((n,)), dma((n,)), dma((n, 7)), dma((n, 7)), dma((n, 8)),
         ],
         compiler_params=pltpu.CompilerParams(vmem_limit_bytes=62 * 2 ** 20, collective_id=0, has_side_effects=True),
-    )(seq_lens, cosine, sine, x_hidden, wq_loc, k_loc, v_loc, wo_loc)
+    )(seq_lens, inv_freq, x_hidden, wq_loc, k_loc, v_loc, wo_loc)
 
 
 def solution(mesh):

time: 94.9 us -> 91 us (0.959)
  Pallas kernels: 90.1 us -> 88 us
  other arithmetic: 1.72 us -> 0 us
    pallas_call x1, Pallas kernels: 90.1 us -> 88 us  [decode(): pl.pallas_call(decode_kernel, out_shape=jax.ShapeDtypeStruct((rows, model...]
where the time goes in v3:
time: 91 us; the launch traced here: 90.7 us
  Pallas kernels  88 us (97%)
  local copies, waits for them, and re-layouts  2.69 us (3%)
    pallas_call x1, Pallas kernels, decode(): pl.pallas_call(decode_kernel, out_shape=jax.ShapeDtypeStruct((rows, model...  88 us
    unnamed x1, local copies, waits for them, and re-layouts  2.69 us

profile of v3, /device:TPU:0, one launch (start us, length us, event | category | flops | bytes accessed | tf_op | source)
XLA Modules:
  0.0 90.7 jit_solution(9332188593538166729)
XLA Ops:
  0.0 88.0 %shard_map.73 = bf16[128,6144]{1,0:T(8,128)(2,1)} custom-call(s32[128]{0:T(128)} %lens_ref.1, f32[1,128]{1,0:T(1,128)} %constant.2.clone.freq_hbm, bf16[128,6144]{1,0:T(8,128)(2,1)} %x_hbm.1, bf16[6,6144,128]{2,1,0:T(8,128)(2,1)} %bitcast.4, bf16[128,2048,128]{2,1,0:T(8,128)(2,1)} %bitcast.1.k_hbm, bf16[128,2048,128]{2,1,0:T(8,128)(2,1)} %bitcast.2.v_hbm, ...), custom_call_target="tpu_custom_call" | custom-call | tf_op jit(solution)/shard_map/pallas_call | solution.py:414
  88.0 2.7 %copy.9 = bf16[128,6144]{1,0:T(8,128)(2,1)} copy(bf16[128,6144]{1,0:T(8,128)(2,1)} %shard_map.73) | data formatting | bytes 3145728
